TPU v7x, 32 devices: a whole 2x2x4 slice. The times are simulated.
32 devices in a mesh: gx: 4 (over y, core), gy: 8 (over z, x).
Axes of the slice: x: 2, y: 2, z: 4, core: 2. Of those that a mesh axis runs over, the one named last changes fastest.
Arguments:
- position: float32 [4, 8, 3, 4096], P('gx', 'gy'), may hold values from 0 to 8, as said below
- velocity: float32 [4, 8, 3, 4096], P('gx', 'gy'), may hold values from -6 to 6
- mass: float32 [4, 8, 1, 4096], P('gx', 'gy'), may hold values from 0.3 to 3
- pair_list: int32 [4, 8, 32, 27], P('gx', 'gy'), may hold values from 0 to 287, as said below
- hot_leaf: int32 [4, 8, 8], P('gx', 'gy'), may hold values from 0 to 32, as said below
Outputs:
- displacement: float32 [4, 8, 3, 4096], P('gx', 'gy')
- new_velocity: float32 [4, 8, 3, 4096], P('gx', 'gy')
Inputs may be any that keep to these rules, and one draw needn't show every extreme that they name: `pair_list`: entry k of every list names a leaf of neighbourhood block k mod 9. `position`: component 0 of a particle of cell (i, j) lies in [i, i + 1), component 1 in [j, j + 1), component 2 in [0, 1). `hot_leaf`: the slots of a cell hold distinct leaf numbers first and the empty mark 32 after them; cell (i, j) and cell (i, (j + 4) mod 8) hold exactly 8 hot leaves together.
All inputs are finite; a program needn't handle non-finite values.
Results may differ from a plain program's by a relative error of at most 0.00023.
Values sent between devices are 32-bit elements; how exact they have to be, the bound alone decides.
A program may use at most 64 MiB of HBM per device.

v0:
```python
import jax
import jax.numpy as jnp
from jax import lax
from jax.sharding import PartitionSpec as P

LEAF = 128


kernel_scale = 1.0
viscosity = 0.5
time_step = 0.5
base_entries = 9


def with_halo(cells, sides, width):
    for axis, dim in sides:
        count = lax.axis_size(axis)
        ends = count - 1
        head = lax.slice_in_dim(cells, 0, width, axis=dim)
        tail = lax.slice_in_dim(cells, cells.shape[dim] - width, cells.shape[dim], axis=dim)
        cells = jnp.concatenate(
            [
                lax.ppermute(tail, axis, [(i, (i + 1) % count) for i in range(ends)]),
                cells,
                lax.ppermute(head, axis, [((i + 1) % count, i) for i in range(ends)]),
            ],
            axis=dim,
        )
    return cells


def source_leaves(extended):
    channels = extended.shape[2]
    count = extended.shape[3] // LEAF
    return jnp.transpose(extended, (2, 0, 1, 3)).reshape(channels, 9 * count, LEAF)


def own_leaves(own):
    channels = own.shape[0]
    count = own.shape[1] // LEAF
    return jnp.transpose(own.reshape(channels, count, LEAF), (1, 0, 2))


def density_part(target, near):
    diff = target[0:3, :, None] - near[0:3, None, :]
    weight = jnp.exp(-jnp.sum(diff * diff, axis=0) / kernel_scale)
    return jnp.sum(near[6][None, :] * weight, axis=1)


def accel_part(target, target_q, near, near_q):
    diff = target[0:3, :, None] - near[0:3, None, :]
    weight = jnp.exp(-jnp.sum(diff * diff, axis=0) / kernel_scale)
    massed = near[6][None, :] * weight
    press = massed * (2.0 / kernel_scale) * (target_q[:, None] + near_q[None, :])
    pushed = jnp.sum(press[None] * diff, axis=2)
    damped = jnp.sum(
        (massed * near_q[None, :])[None] * (near[3:6, None, :] - target[3:6, :, None]), axis=2
    )
    return pushed + viscosity * damped


def surround_state(state):
    return with_halo(state, (("gx", 0), ("gy", 1)), 1)


def surround_density(inverse):
    return with_halo(inverse, (("gx", 0), ("gy", 1)), 1)


def section(position, velocity, mass, pairs, hot):
    leaf_count = pairs.shape[0]
    slots_all = hot.shape[0]
    own = jnp.concatenate([position, velocity, mass], axis=2)
    extended = surround_state(own)
    sources = source_leaves(extended)
    targets = own_leaves(own[0, 0])
    alive = hot < leaf_count
    alive_float = jnp.where(alive, 1.0, 0.0).astype(jnp.float32)
    slot_leaf = jnp.minimum(hot, leaf_count - 1)
    onehot = jnp.where(
        (slot_leaf[:, None] == jnp.arange(leaf_count, dtype=jnp.int32)[None, :]) & alive[:, None],
        1.0,
        0.0,
    ).astype(jnp.float32)

    def base_density(inputs):
        target, chosen = inputs
        near = jnp.take(sources, chosen, axis=1).reshape(sources.shape[0], -1)
        return density_part(target, near)

    base_rho = lax.map(base_density, (targets, pairs[:, :base_entries]))
    extra_chosen = jnp.take(pairs, slot_leaf, axis=0)[:, base_entries:]
    hot_targets = jnp.take(targets, slot_leaf, axis=0)
    hot_near = jnp.transpose(jnp.take(sources, extra_chosen, axis=1), (1, 0, 2, 3)).reshape(
        slots_all, sources.shape[0], -1
    )
    package = jnp.concatenate([hot_targets, hot_near], axis=2) * alive_float[:, None, None]

    def package_density(pack):
        return density_part(pack[:, :LEAF], pack[:, LEAF:])

    def package_accel(inputs):
        pack, qpack = inputs
        return accel_part(pack[:, :LEAF], qpack[:LEAF], pack[:, LEAF:], qpack[LEAF:])

    extra_rho = lax.map(package_density, package)
    extra_rho = extra_rho * alive_float[:, None]
    added_rho = jnp.dot(onehot.T, extra_rho, precision=lax.Precision.HIGHEST)
    inverse_leaves = 1.0 / (targets[:, 6, :] + base_rho + added_rho)
    inverse = inverse_leaves.reshape(1, -1)
    extended_inverse = surround_density(inverse[None, None])
    source_inverse = source_leaves(extended_inverse)[0]

    def base_accel(inputs):
        target, target_q, chosen = inputs
        near = jnp.take(sources, chosen, axis=1).reshape(sources.shape[0], -1)
        near_q = jnp.take(source_inverse, chosen, axis=0).reshape(-1)
        return accel_part(target, target_q, near, near_q)

    base_acc = lax.map(base_accel, (targets, inverse_leaves, pairs[:, :base_entries]))
    hot_q = jnp.take(inverse_leaves, slot_leaf, axis=0)
    near_q = jnp.take(source_inverse, extra_chosen, axis=0).reshape(slots_all, -1)
    qpackage = jnp.concatenate([hot_q, near_q], axis=1) * alive_float[:, None]
    extra_acc = lax.map(package_accel, (package, qpackage))
    extra_acc = extra_acc * alive_float[:, None, None]
    added_acc = jnp.einsum("hl,hcp->lcp", onehot, extra_acc, precision=lax.Precision.HIGHEST)
    total = base_acc + added_acc
    return jnp.transpose(total, (1, 0, 2)).reshape(3, -1)[None, None]


def local(position, velocity, mass, pair_list, hot_leaf):
    pairs = pair_list[0, 0]
    hot = hot_leaf[0, 0]
    first = section(position, velocity, mass, pairs, hot)
    mid_position = position + 0.5 * time_step * velocity
    mid_velocity = velocity + 0.5 * time_step * first
    second = section(mid_position, mid_velocity, mass, pairs, hot)
    return (time_step * mid_velocity, velocity + time_step * second)


def solution(mesh):
    return jax.shard_map(
        local,
        mesh=mesh,
        in_specs=(
            P("gx", "gy", None, None),
            P("gx", "gy", None, None),
            P("gx", "gy", None, None),
            P("gx", "gy", None, None),
            P("gx", "gy", None),
        ),
        out_specs=(P("gx", "gy", None, None), P("gx", "gy", None, None)),
        check_vma=False,
    )
```

profile of v0, /device:TPU:28, one launch (start us, length us, event | category | flops | bytes accessed | tf_op | source)
XLA Modules:
  0.0 379.7 jit_solution(3218418458461015568)
XLA Ops:
  3.6 2.4 collective-permute-start
  11.4 3.3 collective-permute-start.3
  14.7 2.6 collective-permute-start.2
  17.5 12.5 %collective-permute-done.3 = f32[3,1,7,4096]{3,1,2,0:T(1,128)S(1)} collective-permute-done((f32[3,1,7,4096]{3,1,2,0:T(1,128)S(1)}, f32[3,1,7,4096]{3,1,2,0:T(1,128)S(1)}, u32[]{:S(2)}, u32[]{:S(2)}) %collective-permute-start.3) | collective-permute-done | bytes 344096 | tf_op jit(solution)/shard_map/ppermute | solution.py:25
  32.7 38.7 %while.80 = (s32[]{:T(128)}, f32[32,128]{1,0:T(8,128)S(1)}, s32[32,9]{1,0:T(8,128)S(1)}, f32[7,288,128]{2,0,1:T(8,128)S(1)}, f32[32,7,128]{2,1,0:T(8,128)S(1)}, /*index=5*/s32[]{:T(128)}, s32[]{:T(128)}) while((s32[]{:T(128)}, f32[32,128]{1,0:T(8,128)S(1)}, s32[32,9]{1,0:T(8,128)S(1)}, f32[7,288,128]{2,0,1:T(8,128)S(1)}, ...), condition=%wide.region_3.5_spmd, body=%wide.region_0.4_spmd.sunk | while | flops 1631032 | bytes 1381635 | solution.py:91
  72.8 6.5 %while.81 = (s32[]{:T(128)}, f32[8,128]{1,0:T(8,128)S(1)}, f32[8,7,2432]{2,1,0:T(8,128)S(1)}, s32[]{:T(128)}, s32[]{:T(128)}) while((s32[]{:T(128)}, f32[8,128]{1,0:T(8,128)S(1)}, f32[8,7,2432]{2,1,0:T(8,128)S(1)}, s32[]{:T(128)}, s32[]{:T(128)}) %tuple.217), condition=%wide.region_7.12_spmd, body=%wide.region_4.11_spmd.sunk | while | flops 3243906 | bytes 2612301 | solution.py:106
  79.7 3.6 collective-permute-start.5
  85.8 2.6 collective-permute-done.4
  88.4 4.3 %collective-permute-start.7 = (f32[3,1,1,4096]{3,2,1,0:T(1,128)S(1)}, f32[3,1,1,4096]{3,2,1,0:T(1,128)S(1)}, u32[]{:S(2)}, u32[]{:S(2)}) collective-permute-start(f32[3,1,1,4096]{3,2,1,0:T(1,128)S(1)} %pad_maximum_fusion.7), channel_id=1, source_target_pairs={{1,0},{2,1},{3,2},{4,3},{5,4},{6,5},{7,6},{9,8},{10,9},{11,10},{12... | collective-permute-start | bytes 147464 | tf_op jit(solution)/shard_map/ppermute | solution.py:25
  94.7 4.9 %collective-permute-done.6 = f32[3,1,1,4096]{3,2,1,0:T(1,128)S(1)} collective-permute-done((f32[3,1,1,4096]{3,2,1,0:T(1,128)S(1)}, f32[3,1,1,4096]{3,2,1,0:T(1,128)S(1)}, u32[]{:S(2)}, u32[]{:S(2)}) %collective-permute-start.6) | collective-permute-done | bytes 49184 | tf_op jit(solution)/shard_map/ppermute | solution.py:23
  100.4 77.3 %while.82 = (s32[]{:T(128)}, f32[32,3,128]{2,0,1:T(8,128)S(1)}, s32[32,9]{1,0:T(8,128)S(1)}, f32[7,288,128]{2,0,1:T(8,128)S(1)}, f32[32,7,128]{2,1,0:T(8,128)S(1...) while((s32[]{:T(128)}, f32[32,3,128]{2,0,1:T(8,128)S(1)}, ...), condition=%wide.region_12.18_spmd, body=%wide.region_8.17_spmd.sunk | while | flops 4728888 | bytes 3839300 | solution.py:120
  178.0 15.2 %while.83 = (s32[]{:T(128)}, f32[8,3,128]{2,1,0:T(4,128)S(1)}, f32[8,7,2432]{2,1,0:T(8,128)S(1)}, f32[8,2432]{1,0:T(8,128)S(1)}, s32[]{:T(128)}, /*index=5*/s32[]{:T(128)}, s32[]{}) while((s32[]{:T(128)}, f32[8,3,128]{2,1,0:T(4,128)S(1)}, f32[8,7,2432]{2,1,0:T(8,128)S(1)}, f32[8,2432]{1,0:T(8,128)S(1)}, s32[]{:T(128)}, ...), condition=%wide.region_17.25_spmd, body=%wide.region_13.24_spmd.sunk | while | flops 9437187 | bytes 7484533 | solution.py:124
  195.7 2.4 collective-permute-start.8
  198.2 3.8 collective-permute-done.8
  204.0 4.1 %collective-permute-start.10 = (f32[3,1,7,4096]{3,2,1,0:T(8,128)S(1)}, f32[3,1,7,4096]{3,2,1,0:T(8,128)S(1)}, u32[]{:S(2)}, u32[]{:S(2)}) collective-permute-start(f32[3,1,7,4096]{3,2,1,0:T(8,128)S(1)} %pad_maximum_fusion.1), channel_id=1, source_target_pairs={{0,1},{1,2},{2,3},{3,4},{4,5},{5,6},{6,7},{8,9},{9,10},{10,11},{11... | collective-permute-start | bytes 1032200 | tf_op jit(solution)/shard_map/ppermute | solution.py:23
  208.9 12.0 %collective-permute-done.11 = f32[3,1,7,4096]{3,2,1,0:T(8,128)S(1)} collective-permute-done((f32[3,1,7,4096]{3,2,1,0:T(8,128)S(1)}, f32[3,1,7,4096]{3,2,1,0:T(8,128)S(1)}, u32[]{:S(2)}, u32[]{:S(2)}) %collective-permute-start.11) | collective-permute-done | bytes 344096 | tf_op jit(solution)/shard_map/ppermute | solution.py:25
  221.8 38.7 %while.84 = (s32[]{:T(128)}, f32[32,128]{1,0:T(8,128)S(1)}, s32[32,9]{1,0:T(8,128)S(1)}, f32[7,288,128]{2,0,1:T(8,128)S(1)}, f32[32,7,128]{2,1,0:T(8,128)S(1)}, /*index=5*/s32[]{:T(128)}, s32[]{:T(128)}) while((s32[]{:T(128)}, f32[32,128]{1,0:T(8,128)S(1)}, s32[32,9]{1,0:T(8,128)S(1)}, f32[7,288,128]{2,0,1:T(8,128)S(1)}, ...), condition=%wide.region_21.29_spmd, body=%wide.region_18.28_spmd.sunk | while | flops 1631032 | bytes 1381635 | solution.py:91
  261.1 6.5 %while.85 = (s32[]{:T(128)}, f32[8,128]{1,0:T(8,128)S(1)}, f32[8,7,2432]{2,1,0:T(8,128)S(1)}, s32[]{:T(128)}, s32[]{:T(128)}) while((s32[]{:T(128)}, f32[8,128]{1,0:T(8,128)S(1)}, f32[8,7,2432]{2,1,0:T(8,128)S(1)}, s32[]{:T(128)}, s32[]{:T(128)}) %tuple.229), condition=%wide.region_25.33_spmd, body=%wide.region_22.32_spmd.sunk | while | flops 3243906 | bytes 2612301 | solution.py:106
  269.9 2.4 collective-permute-start.12
  275.0 3.1 collective-permute-start.15
  278.1 2.7 collective-permute-start.14
  281.0 4.0 %collective-permute-done.14 = f32[3,1,1,4096]{3,2,1,0:T(1,128)S(1)} collective-permute-done((f32[3,1,1,4096]{3,2,1,0:T(1,128)S(1)}, f32[3,1,1,4096]{3,2,1,0:T(1,128)S(1)}, u32[]{:S(2)}, u32[]{:S(2)}) %collective-permute-start.14) | collective-permute-done | bytes 49184 | tf_op jit(solution)/shard_map/ppermute | solution.py:23
  285.8 77.3 %while.86 = (s32[]{:T(128)}, f32[32,3,128]{2,0,1:T(8,128)S(1)}, s32[32,9]{1,0:T(8,128)S(1)}, f32[7,288,128]{2,0,1:T(8,128)S(1)}, f32[32,7,128]{2,1,0:T(8,128)S(1...) while((s32[]{:T(128)}, f32[32,3,128]{2,0,1:T(8,128)S(1)}, ...), condition=%wide.region_30.38_spmd, body=%wide.region_26.37_spmd.sunk | while | flops 4728888 | bytes 3839300 | solution.py:120
  363.4 15.2 %while.87 = (s32[]{:T(128)}, f32[8,3,128]{2,1,0:T(4,128)S(1)}, f32[8,7,2432]{2,1,0:T(8,128)S(1)}, f32[8,2432]{1,0:T(8,128)S(1)}, s32[]{:T(128)}, /*index=5*/s32[]{:T(128)}, s32[]{}) while((s32[]{:T(128)}, f32[8,3,128]{2,1,0:T(4,128)S(1)}, f32[8,7,2432]{2,1,0:T(8,128)S(1)}, f32[8,2432]{1,0:T(8,128)S(1)}, s32[]{:T(128)}, ...), condition=%wide.region_35.43_spmd, body=%wide.region_31.42_spmd.sunk | while | flops 9437187 | bytes 7484533 | solution.py:124
  (2167 shorter events, 293.3 us)
Async XLA Ops:
  0.6 29.4 %copy-start.2 = (f32[1,1,1,4096]{3,2,1,0:T(1,128)S(1)}, f32[1,1,1,4096]{3,2,1,0:T(1,128)}, u32[]{:S(2)}) copy-start(f32[1,1,1,4096]{3,2,1,0:T(1,128)} %param.37) | copy-start | bytes 49156
  0.6 29.4 %copy-start = (f32[1,1,3,4096]{3,1,2,0:T(1,128)S(1)}, f32[1,1,3,4096]{3,1,2,0:T(1,128)}, u32[]{:S(2)}) copy-start(f32[1,1,3,4096]{3,1,2,0:T(1,128)} %param.36) | copy-start | bytes 147460
  0.7 29.4 %copy-start.1 = (f32[1,1,3,4096]{3,1,2,0:T(1,128)S(1)}, f32[1,1,3,4096]{3,1,2,0:T(1,128)}, u32[]{:S(2)}) copy-start(f32[1,1,3,4096]{3,1,2,0:T(1,128)} %param.35) | copy-start | bytes 147460
  0.7 16.6 %copy-start.3 = (s32[1,1,8]{2,1,0:T(1,128)S(1)}, s32[1,1,8]{2,1,0:T(1,128)}, u32[]{:S(2)}) copy-start(s32[1,1,8]{2,1,0:T(1,128)} %param.39) | copy-start | bytes 100
  1.7 8.6 %collective-permute-start.1 = (f32[1,1,7,4096]{3,1,2,0:T(1,128)S(1)}, f32[1,1,7,4096]{3,1,2,0:T(1,128)S(1)}, u32[]{:S(2)}, u32[]{:S(2)}) collective-permute-start(f32[1,1,7,4096]{3,1,2,0:T(1,128)S(1)} %pad_maximum_fusion.6), channel_id=1, source_target_pairs={{8,0},{16,8},{24,16},{9,1},{17,9},{25,17},{10,2},{18,10},{26,18},{... | collective-permute-start | bytes 344072 | tf_op jit(solution)/shard_map/ppermute | solution.py:25
  3.6 6.6 %collective-permute-start = (f32[1,1,7,4096]{3,1,2,0:T(1,128)S(1)}, f32[1,1,7,4096]{3,1,2,0:T(1,128)S(1)}, u32[]{:S(2)}, u32[]{:S(2)}) collective-permute-start(f32[1,1,7,4096]{3,1,2,0:T(1,128)S(1)} %pad_maximum_fusion.6), channel_id=1, source_target_pairs={{0,8},{8,16},{16,24},{1,9},{9,17},{17,25},{2,10},{10,18},{18,26},{... | collective-permute-start | bytes 344072 | tf_op jit(solution)/shard_map/ppermute | solution.py:23
  11.4 18.6 %collective-permute-start.3 = (f32[3,1,7,4096]{3,1,2,0:T(1,128)S(1)}, f32[3,1,7,4096]{3,1,2,0:T(1,128)S(1)}, u32[]{:S(2)}, u32[]{:S(2)}) collective-permute-start(f32[3,1,7,4096]{3,1,2,0:T(1,128)S(1)} %pad_maximum_fusion.2), channel_id=1, source_target_pairs={{1,0},{2,1},{3,2},{4,3},{5,4},{6,5},{7,6},{9,8},{10,9},{11,10},{12... | collective-permute-start | bytes 1032200 | tf_op jit(solution)/shard_map/ppermute | solution.py:25
  14.7 15.3 %collective-permute-start.2 = (f32[3,1,7,4096]{3,1,2,0:T(1,128)S(1)}, f32[3,1,7,4096]{3,1,2,0:T(1,128)S(1)}, u32[]{:S(2)}, u32[]{:S(2)}) collective-permute-start(f32[3,1,7,4096]{3,1,2,0:T(1,128)S(1)} %pad_maximum_fusion.2), channel_id=1, source_target_pairs={{0,1},{1,2},{2,3},{3,4},{4,5},{5,6},{6,7},{8,9},{9,10},{10,11},{11... | collective-permute-start | bytes 1032200 | tf_op jit(solution)/shard_map/ppermute | solution.py:23
  79.7 6.0 %collective-permute-start.5 = (f32[1,1,1,4096]{3,2,1,0:T(1,128)S(1)}, f32[1,1,1,4096]{3,2,1,0:T(1,128)S(1)}, u32[]{:S(2)}, u32[]{:S(2)}) collective-permute-start(f32[1,1,1,4096]{3,2,1,0:T(1,128)S(1)} %bitcast.260), channel_id=1, source_target_pairs={{8,0},{16,8},{24,16},{9,1},{17,9},{25,17},{10,2},{18,10},{26,18},{... | collective-permute-start | bytes 49160 | tf_op jit(solution)/shard_map/ppermute | solution.py:25
  83.3 5.1 %collective-permute-start.4 = (f32[1,1,1,4096]{3,2,1,0:T(1,128)S(1)}, f32[1,1,1,4096]{3,2,1,0:T(1,128)S(1)}, u32[]{:S(2)}, u32[]{:S(2)}) collective-permute-start(f32[1,1,1,4096]{3,2,1,0:T(1,128)S(1)} %bitcast.261), channel_id=1, source_target_pairs={{0,8},{8,16},{16,24},{1,9},{9,17},{17,25},{2,10},{10,18},{18,26},{... | collective-permute-start | bytes 49160 | tf_op jit(solution)/shard_map/ppermute | solution.py:23
  88.4 6.3 %collective-permute-start.7 = (f32[3,1,1,4096]{3,2,1,0:T(1,128)S(1)}, f32[3,1,1,4096]{3,2,1,0:T(1,128)S(1)}, u32[]{:S(2)}, u32[]{:S(2)}) collective-permute-start(f32[3,1,1,4096]{3,2,1,0:T(1,128)S(1)} %pad_maximum_fusion.7), channel_id=1, source_target_pairs={{1,0},{2,1},{3,2},{4,3},{5,4},{6,5},{7,6},{9,8},{10,9},{11,10},{12... | collective-permute-start | bytes 147464 | tf_op jit(solution)/shard_map/ppermute | solution.py:25
  92.7 6.9 %collective-permute-start.6 = (f32[3,1,1,4096]{3,2,1,0:T(1,128)S(1)}, f32[3,1,1,4096]{3,2,1,0:T(1,128)S(1)}, u32[]{:S(2)}, u32[]{:S(2)}) collective-permute-start(f32[3,1,1,4096]{3,2,1,0:T(1,128)S(1)} %pad_maximum_fusion.7), channel_id=1, source_target_pairs={{0,1},{1,2},{2,3},{3,4},{4,5},{5,6},{6,7},{8,9},{9,10},{10,11},{11... | collective-permute-start | bytes 147464 | tf_op jit(solution)/shard_map/ppermute | solution.py:23
  193.7 4.4 %collective-permute-start.9 = (f32[1,1,7,4096]{3,2,1,0:T(8,128)S(1)}, f32[1,1,7,4096]{3,2,1,0:T(8,128)S(1)}, u32[]{:S(2)}, u32[]{:S(2)}) collective-permute-start(f32[1,1,7,4096]{3,2,1,0:T(8,128)S(1)} %pad_maximum_fusion.5), channel_id=1, source_target_pairs={{8,0},{16,8},{24,16},{9,1},{17,9},{25,17},{10,2},{18,10},{26,18},{... | collective-permute-start | bytes 344072 | tf_op jit(solution)/shard_map/ppermute | solution.py:25
  195.7 6.3 %collective-permute-start.8 = (f32[1,1,7,4096]{3,2,1,0:T(8,128)S(1)}, f32[1,1,7,4096]{3,2,1,0:T(8,128)S(1)}, u32[]{:S(2)}, u32[]{:S(2)}) collective-permute-start(f32[1,1,7,4096]{3,2,1,0:T(8,128)S(1)} %pad_maximum_fusion.5), channel_id=1, source_target_pairs={{0,8},{8,16},{16,24},{1,9},{9,17},{17,25},{2,10},{10,18},{18,26},{... | collective-permute-start | bytes 344072 | tf_op jit(solution)/shard_map/ppermute | solution.py:23
  202.0 18.8 %collective-permute-start.11 = (f32[3,1,7,4096]{3,2,1,0:T(8,128)S(1)}, f32[3,1,7,4096]{3,2,1,0:T(8,128)S(1)}, u32[]{:S(2)}, u32[]{:S(2)}) collective-permute-start(f32[3,1,7,4096]{3,2,1,0:T(8,128)S(1)} %pad_maximum_fusion.1), channel_id=1, source_target_pairs={{1,0},{2,1},{3,2},{4,3},{5,4},{6,5},{7,6},{9,8},{10,9},{11,10},{12... | collective-permute-start | bytes 1032200 | tf_op jit(solution)/shard_map/ppermute | solution.py:25
  204.0 16.9 %collective-permute-start.10 = (f32[3,1,7,4096]{3,2,1,0:T(8,128)S(1)}, f32[3,1,7,4096]{3,2,1,0:T(8,128)S(1)}, u32[]{:S(2)}, u32[]{:S(2)}) collective-permute-start(f32[3,1,7,4096]{3,2,1,0:T(8,128)S(1)} %pad_maximum_fusion.1), channel_id=1, source_target_pairs={{0,1},{1,2},{2,3},{3,4},{4,5},{5,6},{6,7},{8,9},{9,10},{10,11},{11... | collective-permute-start | bytes 1032200 | tf_op jit(solution)/shard_map/ppermute | solution.py:23
  268.0 5.6 %collective-permute-start.13 = (f32[1,1,1,4096]{3,2,1,0:T(1,128)S(1)}, f32[1,1,1,4096]{3,2,1,0:T(1,128)S(1)}, u32[]{:S(2)}, u32[]{:S(2)}) collective-permute-start(f32[1,1,1,4096]{3,2,1,0:T(1,128)S(1)} %bitcast.256), channel_id=1, source_target_pairs={{8,0},{16,8},{24,16},{9,1},{17,9},{25,17},{10,2},{18,10},{26,18},{... | collective-permute-start | bytes 49160 | tf_op jit(solution)/shard_map/ppermute | solution.py:25
  269.9 5.1 %collective-permute-start.12 = (f32[1,1,1,4096]{3,2,1,0:T(1,128)S(1)}, f32[1,1,1,4096]{3,2,1,0:T(1,128)S(1)}, u32[]{:S(2)}, u32[]{:S(2)}) collective-permute-start(f32[1,1,1,4096]{3,2,1,0:T(1,128)S(1)} %bitcast.257), channel_id=1, source_target_pairs={{0,8},{8,16},{16,24},{1,9},{9,17},{17,25},{2,10},{10,18},{18,26},{... | collective-permute-start | bytes 49160 | tf_op jit(solution)/shard_map/ppermute | solution.py:23
  275.0 6.0 %collective-permute-start.15 = (f32[3,1,1,4096]{3,2,1,0:T(1,128)S(1)}, f32[3,1,1,4096]{3,2,1,0:T(1,128)S(1)}, u32[]{:S(2)}, u32[]{:S(2)}) collective-permute-start(f32[3,1,1,4096]{3,2,1,0:T(1,128)S(1)} %pad_maximum_fusion.8), channel_id=1, source_target_pairs={{1,0},{2,1},{3,2},{4,3},{5,4},{6,5},{7,6},{9,8},{10,9},{11,10},{12... | collective-permute-start | bytes 147464 | tf_op jit(solution)/shard_map/ppermute | solution.py:25
  278.1 6.9 %collective-permute-start.14 = (f32[3,1,1,4096]{3,2,1,0:T(1,128)S(1)}, f32[3,1,1,4096]{3,2,1,0:T(1,128)S(1)}, u32[]{:S(2)}, u32[]{:S(2)}) collective-permute-start(f32[3,1,1,4096]{3,2,1,0:T(1,128)S(1)} %pad_maximum_fusion.8), channel_id=1, source_target_pairs={{0,1},{1,2},{2,3},{3,4},{4,5},{5,6},{6,7},{8,9},{9,10},{10,11},{11... | collective-permute-start | bytes 147464 | tf_op jit(solution)/shard_map/ppermute | solution.py:23
where the time goes:
time: 380 us
  other arithmetic  146 us (38%)
  local copies, waits for them, and re-layouts  133 us (35%)
  starting transfers between devices  42.4 us (11%)
  waiting for transfers between devices  41.3 us (11%)
  loops' own time  14.4 us (4%)
    reduce_sum x80, other arithmetic, accel_part(): pushed = jnp.sum(press[None] * diff, axis=2)  47.5 us
    gather x64, local copies, waits for them, and re-layouts, base_accel(): near_q = jnp.take(source_inverse, chosen, axis=0).reshape(-1)  35.6 us
    gather x64, local copies, waits for them, and re-layouts, base_accel(): near = jnp.take(sources, chosen, axis=1).reshape(sources.shape[0], -1)  35.6 us
    gather x64, local copies, waits for them, and re-layouts, base_density(): near = jnp.take(sources, chosen, axis=1).reshape(sources.shape[0], -1)  35.6 us
    ppermute x8, waiting for transfers between devices, with_halo(): lax.ppermute(head, axis, [((i + 1) % count, i) for i in range(ends)])  24.7 us
    ppermute x8, starting transfers between devices, with_halo(): lax.ppermute(head, axis, [((i + 1) % count, i) for i in range(ends)])  21.9 us
    reduce_sum x80, other arithmetic, density_part(): weight = jnp.exp(-jnp.sum(diff * diff, axis=0) / kernel_scale)  21.7 us
    reduce_sum x80, other arithmetic, accel_part(): weight = jnp.exp(-jnp.sum(diff * diff, axis=0) / kernel_scale)  21.7 us
  transfers between devices with their start and end apart: 16, of which 9 were waited for; matrix products, arithmetic and copies ran while one was open for 2% of the time, Pallas kernels for 0%

commit v1 on v0

v1 whole, which is shorter than its diff:
```python
import functools

import jax
import jax.numpy as jnp
from jax import lax
from jax.experimental import pallas as pl
from jax.experimental.pallas import tpu as pltpu
from jax.sharding import PartitionSpec as P

LEAF = 128

kernel_scale = 1.0
viscosity = 0.5
time_step = 0.5
base_entries = 9
COORD = (2.0 * 1.4426950408889634 / kernel_scale) ** 0.5


def with_halo(cells, sides, width):
    for axis, dim in sides:
        count = lax.axis_size(axis)
        ends = count - 1
        head = lax.slice_in_dim(cells, 0, width, axis=dim)
        tail = lax.slice_in_dim(cells, cells.shape[dim] - width, cells.shape[dim], axis=dim)
        cells = jnp.concatenate(
            [
                lax.ppermute(tail, axis, [(i, (i + 1) % count) for i in range(ends)]),
                cells,
                lax.ppermute(head, axis, [((i + 1) % count, i) for i in range(ends)]),
            ],
            axis=dim,
        )
    return cells


def surround(cell):
    extended = with_halo(cell, (("gx", 0), ("gy", 1)), 1)
    return extended.reshape((9,) + extended.shape[2:])


def split3(value):
    first = value.astype(jnp.bfloat16).astype(jnp.float32)
    rest = value - first
    second = rest.astype(jnp.bfloat16).astype(jnp.float32)
    third = (rest - second).astype(jnp.bfloat16).astype(jnp.float32)
    return first, second, third


def coordinate_rows(x, ones_first):
    a = COORD * x
    c = -0.5 * jnp.sum(a * a, axis=0, keepdims=True)
    one = jnp.ones_like(c)
    pad = jnp.zeros_like(a)
    return jnp.concatenate([a, one, c, pad] if ones_first else [a, c, one, pad], axis=0)


def pair_sums(sections, counts, src_ref, leaf_ref, live_ref, *refs):
    place_refs, channel_refs = refs[:sections], refs[sections : 2 * sections]
    out_refs = refs[2 * sections : 3 * sections]
    feature, target, channel = refs[3 * sections :]
    base_items, entries = counts
    blocks, _, width = place_refs[0].shape
    step = min(width, 8 * LEAF)
    own = blocks // 2
    for place_ref, channel_ref, out_ref in zip(place_refs, channel_refs, out_refs):
        for block in range(blocks):

            def prepare(i, carry):
                span = pl.ds(pl.multiple_of(i * step, step), step)
                rows = coordinate_rows(place_ref[block, 0:3, span], True)
                s1, s2, s3 = split3(rows)
                feature[block, :, span] = jnp.concatenate(
                    [s1, s2, s1, s2, s3, s1], axis=0
                ).astype(jnp.bfloat16)
                c1, c2, _ = split3(channel_ref[block, :, span])
                channel[block, :, span] = jnp.concatenate([c1, c2], axis=0).astype(jnp.bfloat16)
                return carry

            lax.fori_loop(0, width // step, prepare, 0)

        def prepare_target(i, carry):
            span = pl.ds(pl.multiple_of(i * LEAF, LEAF), LEAF)
            rows = coordinate_rows(place_ref[own, 0:3, span], False)
            t1, t2, t3 = split3(rows)
            stack = jnp.concatenate(
                [t1, t1, t2, t2, t1, t3, jnp.zeros((LEAF - 48, LEAF), jnp.float32)], axis=0
            )
            target[i] = stack.T.astype(jnp.bfloat16)
            return carry

        lax.fori_loop(0, width // LEAF, prepare_target, 0)

        def sums(item):
            leaf = leaf_ref[item]
            spans = [
                pl.ds(pl.multiple_of(src_ref[item * entries + k] * LEAF, LEAF), LEAF)
                for k in range(entries)
            ]
            near = jnp.concatenate([feature[k, :, spans[k]] for k in range(entries)], axis=1)
            exponent = jnp.dot(
                target[leaf][:, 0:48], near, preferred_element_type=jnp.float32
            )
            weight = jnp.exp2(exponent).astype(jnp.bfloat16)
            rows = jnp.concatenate([channel[k, :, spans[k]] for k in range(entries)], axis=1)
            both = lax.dot_general(
                rows, weight, (((1,), (1,)), ((), ())), preferred_element_type=jnp.float32
            )
            return leaf, both[0:8] + both[8:16]

        def base(i, carry):
            for u in range(4):
                leaf, value = sums(i * 4 + u)
                out_ref[leaf] = value
            return carry

        lax.fori_loop(0, base_items // 4, base, 0)

        def extra(i, carry):
            leaf, first = sums(base_items + 2 * i)
            _, second = sums(base_items + 2 * i + 1)
            out_ref[leaf] = out_ref[leaf] + (first + second)
            return carry

        lax.fori_loop(0, live_ref[0], extra, 0)


def all_sums(tables, places, channels):
    src, leaves, live, base_items = tables
    sections = len(places)
    blocks, _, width = places[0].shape
    count = width // LEAF
    smem = pl.BlockSpec(memory_space=pltpu.SMEM)
    vmem = pl.BlockSpec(memory_space=pltpu.VMEM)
    outs = pl.pallas_call(
        functools.partial(pair_sums, sections, (base_items, base_entries)),
        out_shape=[jax.ShapeDtypeStruct((count, 8, LEAF), jnp.float32)] * sections,
        in_specs=[smem] * 3 + [vmem] * (2 * sections),
        out_specs=[vmem] * sections,
        scratch_shapes=[
            pltpu.VMEM((blocks, 48, width), jnp.bfloat16),
            pltpu.VMEM((count, LEAF, LEAF), jnp.bfloat16),
            pltpu.VMEM((blocks, 16, width), jnp.bfloat16),
        ],
    )(src, leaves, live, *places, *channels)
    return [jnp.transpose(out, (1, 0, 2)).reshape(8, width) for out in outs]


def local(position, velocity, mass, pair_list, hot_leaf):
    pairs = pair_list[0, 0]
    hot = hot_leaf[0, 0]
    leaf_count, listed = pairs.shape
    groups = listed // base_entries
    lists = (pairs % leaf_count).reshape(leaf_count, groups, base_entries)
    alive = hot < leaf_count
    slot_leaf = jnp.minimum(hot, leaf_count - 1)
    extra_src = jnp.take(lists, slot_leaf, axis=0)[:, 1:]
    src = jnp.concatenate([lists[:, 0].reshape(-1), extra_src.reshape(-1)])
    leaves = jnp.concatenate(
        [jnp.arange(leaf_count, dtype=jnp.int32), jnp.repeat(slot_leaf, groups - 1)]
    )
    live = jnp.sum(alive.astype(jnp.int32)).reshape(1)
    tables = (src, leaves, live, leaf_count)

    centre = jnp.stack(
        [
            lax.axis_index("gx").astype(jnp.float32) + 0.5,
            lax.axis_index("gy").astype(jnp.float32) + 0.5,
            jnp.float32(0.5),
        ]
    ).reshape(1, 3, 1)
    own = blocks_own = base_entries // 2
    state = surround(jnp.concatenate([position, velocity, mass], axis=2))
    pos, vel, m = state[:, 0:3], state[:, 3:6], state[:, 6:7]
    x1 = pos - centre
    x2 = (pos + 0.5 * time_step * vel) - centre
    zeros7 = jnp.zeros((m.shape[0], 7, m.shape[2]), jnp.float32)
    mass_rows = jnp.concatenate([m, zeros7], axis=1)
    rho1, rho2 = all_sums(tables, [x1, x2], [mass_rows, mass_rows])
    own_m = mass[0, 0]
    q_own = 1.0 / (own_m + jnp.concatenate([rho1[0:1], rho2[0:1]], axis=0))
    q_all = surround(q_own[None, None])

    def acceleration(x, v, own_v, q, own_q):
        mq = m * q
        rows = jnp.concatenate([m, m * x, mq, mq * (viscosity * v - (2.0 / kernel_scale) * x)], axis=1)
        (s,) = all_sums(tables, [x], [rows])
        own_x = x[own]
        pushed = (2.0 / kernel_scale) * (
            own_q * (own_x * s[0:1] - s[1:4]) + own_x * s[4:5]
        )
        return pushed - viscosity * own_v * s[4:5] + s[5:8]

    own_v = velocity[0, 0]
    acc1 = acceleration(x1, vel, own_v, q_all[:, 0:1], q_own[0:1])
    mid_velocity = own_v + 0.5 * time_step * acc1
    mid_all = surround(mid_velocity[None, None])
    acc2 = acceleration(x2, mid_all, mid_velocity, q_all[:, 1:2], q_own[1:2])
    return (
        (time_step * mid_velocity)[None, None],
        (own_v + time_step * acc2)[None, None],
    )


def solution(mesh):
    return jax.shard_map(
        local,
        mesh=mesh,
        in_specs=(
            P("gx", "gy", None, None),
            P("gx", "gy", None, None),
            P("gx", "gy", None, None),
            P("gx", "gy", None, None),
            P("gx", "gy", None),
        ),
        out_specs=(P("gx", "gy", None, None), P("gx", "gy", None, None)),
        check_vma=False,
    )
```

time: 380 us -> 159 us (0.42)
  other arithmetic: 146 us -> 15.9 us
  local copies, waits for them, and re-layouts: 133 us -> 7.74 us
  Pallas kernels: 0 us -> 75.3 us
  waiting for transfers between devices: 41.3 us -> 19.3 us
  loops' own time: 14.4 us -> 0 us
  starting transfers between devices: 42.4 us -> 37.1 us
    gather x203 -> x1, local copies, waits for them, and re-layouts: 112 us -> 0.58 us  [local(): extra_src = jnp.take(lists, slot_leaf, axis=0)[:, 1:]]
    reduce_sum x320 -> x1, other arithmetic: 106 us -> 0.65 us  [local(): live = jnp.sum(alive.astype(jnp.int32)).reshape(1)]
    pallas_call x0 -> x3, Pallas kernels: none -> 75.3 us  [all_sums(): pl.pallas_call(functools.partial(pair_sums, sections, (base_items, base_e...]
    another operation x8 -> x0, loops' own time: 14.4 us -> none  [the longest x2 7.24 us: section(): lax.map(base_accel, (targets, inverse_leaves, pairs[:, :base_entries]))]
    ppermute x8 -> x6, waiting for transfers between devices: 16.6 us -> 4.03 us  [with_halo(): lax.ppermute(tail, axis, [(i, (i + 1) % count) for i in range(ends)])]
    mul x88 -> x8, other arithmetic: 15.5 us -> 3.91 us  [the longest x1 1.7 us: acceleration(): m * x]
    select_n x135 -> x3, other arithmetic: 11 us -> 0.79 us  [the longest x2 0.74 us: local(): extra_src = jnp.take(lists, slot_leaf, axis=0)[:, 1:]]
    ppermute x8 -> x6, waiting for transfers between devices: 24.7 us -> 15.2 us  [with_halo(): lax.ppermute(head, axis, [((i + 1) % count, i) for i in range(ends)])]
  transfers between devices with their start and end apart: 16 -> 12, of which waited for: 9 -> 8; matrix products, arithmetic and copies ran while one was open for 2% -> 4% of each run, Pallas kernels for 0% -> 0%
where the time goes in v1:
time: 159 us; the launch traced here: 156 us
  Pallas kernels  75.3 us (47%)
  starting transfers between devices  37.1 us (23%)
  waiting for transfers between devices  19.3 us (12%)
  other arithmetic  15.9 us (10%)
  local copies, waits for them, and re-layouts  7.74 us (5%)
    pallas_call x3, Pallas kernels, all_sums(): pl.pallas_call(functools.partial(pair_sums, sections, (base_items, base_e...  75.3 us
    ppermute x6, starting transfers between devices, with_halo(): lax.ppermute(head, axis, [((i + 1) % count, i) for i in range(ends)])  24.1 us
    ppermute x6, waiting for transfers between devices, with_halo(): lax.ppermute(head, axis, [((i + 1) % count, i) for i in range(ends)])  15.2 us
    ppermute x6, starting transfers between devices, with_halo(): lax.ppermute(tail, axis, [(i, (i + 1) % count) for i in range(ends)])  13 us
    ppermute x6, waiting for transfers between devices, with_halo(): lax.ppermute(tail, axis, [(i, (i + 1) % count) for i in range(ends)])  4.03 us
    concatenate x2, other arithmetic, acceleration(): jnp.concatenate([m, m * x, mq, mq * (viscosity * v - 2.0 / kernel_scale *...  3.19 us
  transfers between devices with their start and end apart: 12, of which 8 were waited for; matrix products, arithmetic and copies ran while one was open for 4% of the time, Pallas kernels for 0%

profile of v1, /device:TPU:28, one launch (start us, length us, event | category | flops | bytes accessed | tf_op | source)
XLA Modules:
  0.0 156.2 jit_solution(7965683278795049770)
XLA Ops:
  1.7 1.9 %collective-permute-start = (f32[1,1,7,4096]{3,1,2,0:T(1,128)S(1)}, f32[1,1,7,4096]{3,1,2,0:T(1,128)S(1)}, u32[]{:S(2)}, u32[]{:S(2)}) collective-permute-start(f32[1,1,7,4096]{3,1,2,0:T(1,128)S(1)} %pad_maximum_fusion.6), channel_id=1, source_target_pairs={{0,8},{8,16},{16,24},{1,9},{9,17},{17,25},{2,10},{10,18},{18,26},{... | collective-permute-start | bytes 344072 | tf_op jit(solution)/shard_map/ppermute | solution.py:27
  3.6 3.6 %collective-permute-start.1 = (f32[1,1,7,4096]{3,1,2,0:T(1,128)S(1)}, f32[1,1,7,4096]{3,1,2,0:T(1,128)S(1)}, u32[]{:S(2)}, u32[]{:S(2)}) collective-permute-start(f32[1,1,7,4096]{3,1,2,0:T(1,128)S(1)} %pad_maximum_fusion.6), channel_id=1, source_target_pairs={{8,0},{16,8},{24,16},{9,1},{17,9},{25,17},{10,2},{18,10},{26,18},{... | collective-permute-start | bytes 344072 | tf_op jit(solution)/shard_map/ppermute | solution.py:29
  11.4 3.4 %collective-permute-start.2 = (f32[3,1,7,4096]{3,1,2,0:T(1,128)S(1)}, f32[3,1,7,4096]{3,1,2,0:T(1,128)S(1)}, u32[]{:S(2)}, u32[]{:S(2)}) collective-permute-start(f32[3,1,7,4096]{3,1,2,0:T(1,128)S(1)} %pad_maximum_fusion.3), channel_id=1, source_target_pairs={{0,1},{1,2},{2,3},{3,4},{4,5},{5,6},{6,7},{8,9},{9,10},{10,11},{11... | collective-permute-start | bytes 1032200 | tf_op jit(solution)/shard_map/ppermute | solution.py:27
  14.8 3.3 %collective-permute-start.3 = (f32[3,1,7,4096]{3,1,2,0:T(1,128)S(1)}, f32[3,1,7,4096]{3,1,2,0:T(1,128)S(1)}, u32[]{:S(2)}, u32[]{:S(2)}) collective-permute-start(f32[3,1,7,4096]{3,1,2,0:T(1,128)S(1)} %pad_maximum_fusion.3), channel_id=1, source_target_pairs={{1,0},{2,1},{3,2},{4,3},{5,4},{6,5},{7,6},{9,8},{10,9},{11,10},{12... | collective-permute-start | bytes 1032200 | tf_op jit(solution)/shard_map/ppermute | solution.py:29
  20.5 2.5 %collective-permute-done.2 = f32[3,1,7,4096]{3,1,2,0:T(1,128)S(1)} collective-permute-done((f32[3,1,7,4096]{3,1,2,0:T(1,128)S(1)}, f32[3,1,7,4096]{3,1,2,0:T(1,128)S(1)}, u32[]{:S(2)}, u32[]{:S(2)}) %collective-permute-start.2) | collective-permute-done | bytes 344096 | tf_op jit(solution)/shard_map/ppermute | solution.py:27
  23.1 7.3 %collective-permute-done.3 = f32[3,1,7,4096]{3,1,2,0:T(1,128)S(1)} collective-permute-done((f32[3,1,7,4096]{3,1,2,0:T(1,128)S(1)}, f32[3,1,7,4096]{3,1,2,0:T(1,128)S(1)}, u32[]{:S(2)}, u32[]{:S(2)}) %collective-permute-start.3) | collective-permute-done | bytes 344096 | tf_op jit(solution)/shard_map/ppermute | solution.py:29
  33.4 1.7 %broadcast_multiply_fusion = (f32[9,3,4096]{2,1,0:T(4,128)S(1)}, f32[9,3,4096]{2,1,0:T(4,128)}, f32[9,3,4096]{2,1,0:T(4,128)S(1)}, f32[9,3,4096]{2,1,0:T(4,128)}) fusion(f32[9,4096]{1,0:T(8,128)S(1)} %bitcast.102, f32[3]{0:T(128)S(1)} %pad_maximum_fusion.8, f32[9,7,4096]{2,1,0:T(8,128)S(1)} %bitcast.98), kind=kLoop, calls=%fused_computation.16 | loop fusion | flops 663552 | bytes 2801676 | tf_op jit(solution)/shard_map/mul | solution.py:185
  35.1 36.5 %shard_map.68 = (f32[32,8,128]{2,1,0:T(8,128)}, f32[32,8,128]{2,1,0:T(8,128)}) custom-call(s32[432]{0:T(512)} %pad_add_fusion.src_ref, s32[48]{0:T(128)} %pad_add_fusion.1.leaf_ref, s32[1]{0:T(128)} %bitcast.4.live_ref, f32[9,3,4096]{2,1,0:T(4,128)} %get-tuple-element.19.refs_0_, f32[9,3,4096]{2,1,0:T(4,128)} %get-tuple-element.11.refs_1_.refs_0_, ...), custom_call_target="tpu_custom_call" | custom-call | tf_op jit(solution)/shard_map/pallas_call | solution.py:134
  72.7 1.9 %collective-permute-start.4 = (f32[1,1,2,4096]{3,2,1,0:T(2,128)S(1)}, f32[1,1,2,4096]{3,2,1,0:T(2,128)S(1)}, u32[]{:S(2)}, u32[]{:S(2)}) collective-permute-start(f32[1,1,2,4096]{3,2,1,0:T(2,128)S(1)} %fusion.21), channel_id=1, source_target_pairs={{0,8},{8,16},{16,24},{1,9},{9,17},{17,25},{2,10},{10,18},{18,26},{... | collective-permute-start | bytes 98312 | tf_op jit(solution)/shard_map/ppermute | solution.py:27
  74.7 3.6 %collective-permute-start.5 = (f32[1,1,2,4096]{3,2,1,0:T(2,128)S(1)}, f32[1,1,2,4096]{3,2,1,0:T(2,128)S(1)}, u32[]{:S(2)}, u32[]{:S(2)}) collective-permute-start(f32[1,1,2,4096]{3,2,1,0:T(2,128)S(1)} %fusion.21), channel_id=1, source_target_pairs={{8,0},{16,8},{24,16},{9,1},{17,9},{25,17},{10,2},{18,10},{26,18},{... | collective-permute-start | bytes 98312 | tf_op jit(solution)/shard_map/ppermute | solution.py:29
  78.4 1.5 collective-permute-done.5
  79.9 1.9 %collective-permute-start.6 = (f32[3,1,2,4096]{3,2,1,0:T(2,128)S(1)}, f32[3,1,2,4096]{3,2,1,0:T(2,128)S(1)}, u32[]{:S(2)}, u32[]{:S(2)}) collective-permute-start(f32[3,1,2,4096]{3,2,1,0:T(2,128)S(1)} %pad_maximum_fusion.7), channel_id=1, source_target_pairs={{0,1},{1,2},{2,3},{3,4},{4,5},{5,6},{6,7},{8,9},{9,10},{10,11},{11... | collective-permute-start | bytes 294920 | tf_op jit(solution)/shard_map/ppermute | solution.py:27
  81.9 4.8 %collective-permute-start.7 = (f32[3,1,2,4096]{3,2,1,0:T(2,128)S(1)}, f32[3,1,2,4096]{3,2,1,0:T(2,128)S(1)}, u32[]{:S(2)}, u32[]{:S(2)}) collective-permute-start(f32[3,1,2,4096]{3,2,1,0:T(2,128)S(1)} %pad_maximum_fusion.7), channel_id=1, source_target_pairs={{1,0},{2,1},{3,2},{4,3},{5,4},{6,5},{7,6},{9,8},{10,9},{11,10},{12... | collective-permute-start | bytes 294920 | tf_op jit(solution)/shard_map/ppermute | solution.py:29
  87.4 1.5 collective-permute-done.7
  89.8 1.6 %fusion.1.refs_1_ = f32[9,8,4096]{2,1,0:T(8,128)} fusion(f32[9,1,4096]{2,1,0:T(1,128)S(1)} %slice.120, f32[9,3,4096]{2,1,0:T(4,128)S(1)} %subtract_multiply_fusion, f32[9,1,4096]{2,1,0:T(1,128)S(1)} %get-tuple-element.17, f32[9,3,4096]{2,1,0:T(4,128)S(1)} %get-tuple-element.18), kind=kLoop, calls=%fused_computation.5 | loop fusion | flops 884736 | bytes 2359296 | tf_op jit(solution)/shard_map/concatenate | solution.py:185
  91.4 19.3 %shard_map.69 = f32[32,8,128]{2,1,0:T(8,128)} custom-call(s32[432]{0:T(512)} %pad_add_fusion.src_ref, s32[48]{0:T(128)} %pad_add_fusion.1.leaf_ref, s32[1]{0:T(128)} %bitcast.4.live_ref, f32[9,3,4096]{2,1,0:T(4,128)} %get-tuple-element.19.refs_0_, f32[9,8,4096]{2,1,0:T(8,128)} %fusion.1.refs_1_), custom_call_target="tpu_custom_call" | custom-call | tf_op jit(solution)/shard_map/pallas_call | solution.py:134
  112.9 1.9 %collective-permute-start.8 = (f32[1,1,3,4096]{3,2,1,0:T(4,128)S(1)}, f32[1,1,3,4096]{3,2,1,0:T(4,128)S(1)}, u32[]{:S(2)}, u32[]{:S(2)}) collective-permute-start(f32[1,1,3,4096]{3,2,1,0:T(4,128)S(1)} %get-tuple-element.13), channel_id=1, source_target_pairs={{0,8},{8,16},{16,24},{1,9},{9,17},{17,25},{2,10},{10,18},{18,26},{... | collective-permute-start | bytes 147464 | tf_op jit(solution)/shard_map/ppermute | solution.py:27
  114.8 3.6 %collective-permute-start.9 = (f32[1,1,3,4096]{3,2,1,0:T(4,128)S(1)}, f32[1,1,3,4096]{3,2,1,0:T(4,128)S(1)}, u32[]{:S(2)}, u32[]{:S(2)}) collective-permute-start(f32[1,1,3,4096]{3,2,1,0:T(4,128)S(1)} %get-tuple-element.13), channel_id=1, source_target_pairs={{8,0},{16,8},{24,16},{9,1},{17,9},{25,17},{10,2},{18,10},{26,18},{... | collective-permute-start | bytes 147464 | tf_op jit(solution)/shard_map/ppermute | solution.py:29
  118.5 1.9 %collective-permute-done.9 = f32[1,1,3,4096]{3,2,1,0:T(4,128)S(1)} collective-permute-done((f32[1,1,3,4096]{3,2,1,0:T(4,128)S(1)}, f32[1,1,3,4096]{3,2,1,0:T(4,128)S(1)}, u32[]{:S(2)}, u32[]{:S(2)}) %collective-permute-start.9) | collective-permute-done | bytes 49184 | tf_op jit(solution)/shard_map/ppermute | solution.py:29
  120.4 1.9 %collective-permute-start.10 = (f32[3,1,3,4096]{3,2,1,0:T(4,128)S(1)}, f32[3,1,3,4096]{3,2,1,0:T(4,128)S(1)}, u32[]{:S(2)}, u32[]{:S(2)}) collective-permute-start(f32[3,1,3,4096]{3,2,1,0:T(4,128)S(1)} %pad_maximum_fusion.5), channel_id=1, source_target_pairs={{0,1},{1,2},{2,3},{3,4},{4,5},{5,6},{6,7},{8,9},{9,10},{10,11},{11... | collective-permute-start | bytes 442376 | tf_op jit(solution)/shard_map/ppermute | solution.py:27
  122.4 5.0 %collective-permute-start.11 = (f32[3,1,3,4096]{3,2,1,0:T(4,128)S(1)}, f32[3,1,3,4096]{3,2,1,0:T(4,128)S(1)}, u32[]{:S(2)}, u32[]{:S(2)}) collective-permute-start(f32[3,1,3,4096]{3,2,1,0:T(4,128)S(1)} %pad_maximum_fusion.5), channel_id=1, source_target_pairs={{1,0},{2,1},{3,2},{4,3},{5,4},{6,5},{7,6},{9,8},{10,9},{11,10},{12... | collective-permute-start | bytes 442376 | tf_op jit(solution)/shard_map/ppermute | solution.py:29
  129.0 3.0 %collective-permute-done.11 = f32[3,1,3,4096]{3,2,1,0:T(4,128)S(1)} collective-permute-done((f32[3,1,3,4096]{3,2,1,0:T(4,128)S(1)}, f32[3,1,3,4096]{3,2,1,0:T(4,128)S(1)}, u32[]{:S(2)}, u32[]{:S(2)}) %collective-permute-start.11) | collective-permute-done | bytes 147488 | tf_op jit(solution)/shard_map/ppermute | solution.py:29
  132.5 1.6 %fusion.3.refs_1_ = f32[9,8,4096]{2,1,0:T(8,128)} fusion(f32[9,1,4096]{2,1,0:T(1,128)S(1)} %slice.120, f32[9,3,4096]{2,1,0:T(4,128)S(1)} %fusion.4, f32[9,1,4096]{2,1,0:T(1,128)S(1)} %get-tuple-element.16, f32[9,3,4096]{2,1,0:T(4,128)S(1)} %get-tuple-element.10), kind=kLoop, calls=%fused_computation.7 | loop fusion | flops 884736 | bytes 2359296 | tf_op jit(solution)/shard_map/concatenate | solution.py:185
  134.1 19.4 %shard_map.70 = f32[32,8,128]{2,1,0:T(8,128)} custom-call(s32[432]{0:T(512)} %pad_add_fusion.src_ref, s32[48]{0:T(128)} %pad_add_fusion.1.leaf_ref, s32[1]{0:T(128)} %bitcast.4.live_ref, f32[9,3,4096]{2,1,0:T(4,128)} %get-tuple-element.11.refs_1_.refs_0_, f32[9,8,4096]{2,1,0:T(8,128)} %fusion.3.refs_1_), custom_call_target="tpu_custom_call" | custom-call | tf_op jit(solution)/shard_map/pallas_call | solution.py:134
  (65 shorter events, 20.2 us)
Async XLA Ops:
  0.6 29.7 %copy-start.4 = (f32[1,1,1,4096]{3,2,1,0:T(1,128)S(1)}, f32[1,1,1,4096]{3,2,1,0:T(1,128)}, u32[]{:S(2)}) copy-start(f32[1,1,1,4096]{3,2,1,0:T(1,128)} %param.7) | copy-start | bytes 49156
  0.6 29.7 %copy-start.3 = (f32[1,1,3,4096]{3,1,2,0:T(1,128)S(1)}, f32[1,1,3,4096]{3,1,2,0:T(1,128)}, u32[]{:S(2)}) copy-start(f32[1,1,3,4096]{3,1,2,0:T(1,128)} %param.5) | copy-start | bytes 147460
  0.7 29.7 %copy-start.2 = (f32[1,1,3,4096]{3,1,2,0:T(1,128)S(1)}, f32[1,1,3,4096]{3,1,2,0:T(1,128)}, u32[]{:S(2)}) copy-start(f32[1,1,3,4096]{3,1,2,0:T(1,128)} %param.6) | copy-start | bytes 147460
  0.7 17.5 %copy-start.5 = (s32[1,1,8]{2,1,0:T(1,128)S(1)}, s32[1,1,8]{2,1,0:T(1,128)}, u32[]{:S(2)}) copy-start(s32[1,1,8]{2,1,0:T(1,128)} %param.9) | copy-start | bytes 100
  1.7 8.6 %collective-permute-start = (f32[1,1,7,4096]{3,1,2,0:T(1,128)S(1)}, f32[1,1,7,4096]{3,1,2,0:T(1,128)S(1)}, u32[]{:S(2)}, u32[]{:S(2)}) collective-permute-start(f32[1,1,7,4096]{3,1,2,0:T(1,128)S(1)} %pad_maximum_fusion.6), channel_id=1, source_target_pairs={{0,8},{8,16},{16,24},{1,9},{9,17},{17,25},{2,10},{10,18},{18,26},{... | collective-permute-start | bytes 344072 | tf_op jit(solution)/shard_map/ppermute | solution.py:27
  3.6 6.6 %collective-permute-start.1 = (f32[1,1,7,4096]{3,1,2,0:T(1,128)S(1)}, f32[1,1,7,4096]{3,1,2,0:T(1,128)S(1)}, u32[]{:S(2)}, u32[]{:S(2)}) collective-permute-start(f32[1,1,7,4096]{3,1,2,0:T(1,128)S(1)} %pad_maximum_fusion.6), channel_id=1, source_target_pairs={{8,0},{16,8},{24,16},{9,1},{17,9},{25,17},{10,2},{18,10},{26,18},{... | collective-permute-start | bytes 344072 | tf_op jit(solution)/shard_map/ppermute | solution.py:29
  11.4 11.6 %collective-permute-start.2 = (f32[3,1,7,4096]{3,1,2,0:T(1,128)S(1)}, f32[3,1,7,4096]{3,1,2,0:T(1,128)S(1)}, u32[]{:S(2)}, u32[]{:S(2)}) collective-permute-start(f32[3,1,7,4096]{3,1,2,0:T(1,128)S(1)} %pad_maximum_fusion.3), channel_id=1, source_target_pairs={{0,1},{1,2},{2,3},{3,4},{4,5},{5,6},{6,7},{8,9},{9,10},{10,11},{11... | collective-permute-start | bytes 1032200 | tf_op jit(solution)/shard_map/ppermute | solution.py:27
  14.8 15.5 %collective-permute-start.3 = (f32[3,1,7,4096]{3,1,2,0:T(1,128)S(1)}, f32[3,1,7,4096]{3,1,2,0:T(1,128)S(1)}, u32[]{:S(2)}, u32[]{:S(2)}) collective-permute-start(f32[3,1,7,4096]{3,1,2,0:T(1,128)S(1)} %pad_maximum_fusion.3), channel_id=1, source_target_pairs={{1,0},{2,1},{3,2},{4,3},{5,4},{6,5},{7,6},{9,8},{10,9},{11,10},{12... | collective-permute-start | bytes 1032200 | tf_op jit(solution)/shard_map/ppermute | solution.py:29
  71.6 17.9 %copy-start.1 = (f32[9,3,4096]{2,1,0:T(4,128)S(1)}, f32[9,3,4096]{2,1,0:T(4,128)}, u32[]{:S(2)}) copy-start(f32[9,3,4096]{2,1,0:T(4,128)} %get-tuple-element.19.refs_0_) | copy-start | bytes 1327108
  72.7 5.6 %collective-permute-start.4 = (f32[1,1,2,4096]{3,2,1,0:T(2,128)S(1)}, f32[1,1,2,4096]{3,2,1,0:T(2,128)S(1)}, u32[]{:S(2)}, u32[]{:S(2)}) collective-permute-start(f32[1,1,2,4096]{3,2,1,0:T(2,128)S(1)} %fusion.21), channel_id=1, source_target_pairs={{0,8},{8,16},{16,24},{1,9},{9,17},{17,25},{2,10},{10,18},{18,26},{... | collective-permute-start | bytes 98312 | tf_op jit(solution)/shard_map/ppermute | solution.py:27
  74.7 5.2 %collective-permute-start.5 = (f32[1,1,2,4096]{3,2,1,0:T(2,128)S(1)}, f32[1,1,2,4096]{3,2,1,0:T(2,128)S(1)}, u32[]{:S(2)}, u32[]{:S(2)}) collective-permute-start(f32[1,1,2,4096]{3,2,1,0:T(2,128)S(1)} %fusion.21), channel_id=1, source_target_pairs={{8,0},{16,8},{24,16},{9,1},{17,9},{25,17},{10,2},{18,10},{26,18},{... | collective-permute-start | bytes 98312 | tf_op jit(solution)/shard_map/ppermute | solution.py:29
  79.9 7.4 %collective-permute-start.6 = (f32[3,1,2,4096]{3,2,1,0:T(2,128)S(1)}, f32[3,1,2,4096]{3,2,1,0:T(2,128)S(1)}, u32[]{:S(2)}, u32[]{:S(2)}) collective-permute-start(f32[3,1,2,4096]{3,2,1,0:T(2,128)S(1)} %pad_maximum_fusion.7), channel_id=1, source_target_pairs={{0,1},{1,2},{2,3},{3,4},{4,5},{5,6},{6,7},{8,9},{9,10},{10,11},{11... | collective-permute-start | bytes 294920 | tf_op jit(solution)/shard_map/ppermute | solution.py:27
  81.9 7.0 %collective-permute-start.7 = (f32[3,1,2,4096]{3,2,1,0:T(2,128)S(1)}, f32[3,1,2,4096]{3,2,1,0:T(2,128)S(1)}, u32[]{:S(2)}, u32[]{:S(2)}) collective-permute-start(f32[3,1,2,4096]{3,2,1,0:T(2,128)S(1)} %pad_maximum_fusion.7), channel_id=1, source_target_pairs={{1,0},{2,1},{3,2},{4,3},{5,4},{6,5},{7,6},{9,8},{10,9},{11,10},{12... | collective-permute-start | bytes 294920 | tf_op jit(solution)/shard_map/ppermute | solution.py:29
  111.8 20.4 %copy-start = (f32[9,3,4096]{2,1,0:T(4,128)S(1)}, f32[9,3,4096]{2,1,0:T(4,128)}, u32[]{:S(2)}) copy-start(f32[9,3,4096]{2,1,0:T(4,128)} %get-tuple-element.11.refs_1_.refs_0_) | copy-start | bytes 1327108
  112.9 5.6 %collective-permute-start.8 = (f32[1,1,3,4096]{3,2,1,0:T(4,128)S(1)}, f32[1,1,3,4096]{3,2,1,0:T(4,128)S(1)}, u32[]{:S(2)}, u32[]{:S(2)}) collective-permute-start(f32[1,1,3,4096]{3,2,1,0:T(4,128)S(1)} %get-tuple-element.13), channel_id=1, source_target_pairs={{0,8},{8,16},{16,24},{1,9},{9,17},{17,25},{2,10},{10,18},{18,26},{... | collective-permute-start | bytes 147464 | tf_op jit(solution)/shard_map/ppermute | solution.py:27
  114.8 5.5 %collective-permute-start.9 = (f32[1,1,3,4096]{3,2,1,0:T(4,128)S(1)}, f32[1,1,3,4096]{3,2,1,0:T(4,128)S(1)}, u32[]{:S(2)}, u32[]{:S(2)}) collective-permute-start(f32[1,1,3,4096]{3,2,1,0:T(4,128)S(1)} %get-tuple-element.13), channel_id=1, source_target_pairs={{8,0},{16,8},{24,16},{9,1},{17,9},{25,17},{10,2},{18,10},{26,18},{... | collective-permute-start | bytes 147464 | tf_op jit(solution)/shard_map/ppermute | solution.py:29
  120.4 8.6 %collective-permute-start.10 = (f32[3,1,3,4096]{3,2,1,0:T(4,128)S(1)}, f32[3,1,3,4096]{3,2,1,0:T(4,128)S(1)}, u32[]{:S(2)}, u32[]{:S(2)}) collective-permute-start(f32[3,1,3,4096]{3,2,1,0:T(4,128)S(1)} %pad_maximum_fusion.5), channel_id=1, source_target_pairs={{0,1},{1,2},{2,3},{3,4},{4,5},{5,6},{6,7},{8,9},{9,10},{10,11},{11... | collective-permute-start | bytes 442376 | tf_op jit(solution)/shard_map/ppermute | solution.py:27
  122.4 9.7 %collective-permute-start.11 = (f32[3,1,3,4096]{3,2,1,0:T(4,128)S(1)}, f32[3,1,3,4096]{3,2,1,0:T(4,128)S(1)}, u32[]{:S(2)}, u32[]{:S(2)}) collective-permute-start(f32[3,1,3,4096]{3,2,1,0:T(4,128)S(1)} %pad_maximum_fusion.5), channel_id=1, source_target_pairs={{1,0},{2,1},{3,2},{4,3},{5,4},{6,5},{7,6},{9,8},{10,9},{11,10},{12... | collective-permute-start | bytes 442376 | tf_op jit(solution)/shard_map/ppermute | solution.py:29

commit v2 on v1

--- a/solution.py
+++ b/solution.py
@@ -8,6 +8,7 @@
 from jax.sharding import PartitionSpec as P
 
 LEAF = 128
+MESH = pl.DeviceIdType.MESH
 
 kernel_scale = 1.0
 viscosity = 0.5
@@ -16,26 +17,85 @@
 COORD = (2.0 * 1.4426950408889634 / kernel_scale) ** 0.5
 
 
-def with_halo(cells, sides, width):
-    for axis, dim in sides:
-        count = lax.axis_size(axis)
-        ends = count - 1
-        head = lax.slice_in_dim(cells, 0, width, axis=dim)
-        tail = lax.slice_in_dim(cells, cells.shape[dim] - width, cells.shape[dim], axis=dim)
-        cells = jnp.concatenate(
-            [
-                lax.ppermute(tail, axis, [(i, (i + 1) % count) for i in range(ends)]),
-                cells,
-                lax.ppermute(head, axis, [((i + 1) % count, i) for i in range(ends)]),
-            ],
-            axis=dim,
+def exchange(sizes, own_ref, out_ref, send_sem, recv_sem):
+    count_x, count_y = sizes
+    gx, gy = lax.axis_index("gx"), lax.axis_index("gy")
+
+    def inside(a, b):
+        terms = []
+        if a != 1:
+            terms.append(gx > 0 if a == 0 else gx < count_x - 1)
+        if b != 1:
+            terms.append(gy > 0 if b == 0 else gy < count_y - 1)
+        return terms[0] if len(terms) == 1 else terms[0] & terms[1]
+
+    def device(a, b):
+        return (jnp.clip(gx + a - 1, 0, count_x - 1), jnp.clip(gy + b - 1, 0, count_y - 1))
+
+    sides = ((1, 0), (1, 2), (0, 1), (2, 1))
+    barrier = pltpu.get_barrier_semaphore()
+    for a, b in sides:
+
+        @pl.when(inside(a, b))
+        def _():
+            pl.semaphore_signal(barrier, inc=1, device_id=device(a, b), device_id_type=MESH)
+
+    pl.semaphore_wait(barrier, sum(inside(a, b).astype(jnp.int32) for a, b in sides))
+
+    def copy(source, block, to):
+        return pltpu.make_async_remote_copy(
+            src_ref=source,
+            dst_ref=out_ref.at[block],
+            send_sem=send_sem.at[block],
+            recv_sem=recv_sem.at[block],
+            device_id=device(*to),
+            device_id_type=MESH,
         )
-    return cells
-
-
-def surround(cell):
-    extended = with_halo(cell, (("gx", 0), ("gy", 1)), 1)
-    return extended.reshape((9,) + extended.shape[2:])
+
+    def sent(a, b):
+        to = (1, 2 - b) if a == 1 else (2 - a, 1)
+        source = own_ref if a == 1 or b == 1 else out_ref.at[3 + b]
+        return copy(source, 3 * a + b, to), inside(*to) if a == 1 or b == 1 else inside(2 - a, b)
+
+    for a, b in sides:
+        descriptor, valid = sent(a, b)
+        pl.when(valid)(descriptor.start)
+    out_ref[4] = own_ref[...]
+    for a in range(3):
+        for b in range(3):
+            if (a, b) != (1, 1):
+
+                @pl.when(jnp.logical_not(inside(a, b)))
+                def _():
+                    out_ref[3 * a + b] = jnp.zeros(own_ref.shape, own_ref.dtype)
+
+    for b in (0, 2):
+        pl.when(inside(1, b))(sent(1, b)[0].wait_recv)
+        for a in (0, 2):
+            descriptor, valid = sent(a, b)
+            pl.when(valid)(descriptor.start)
+    for a, b in ((0, 1), (2, 1), (0, 0), (2, 0), (0, 2), (2, 2)):
+        pl.when(inside(a, b))(sent(a, b)[0].wait_recv)
+    for a in range(3):
+        for b in range(3):
+            if (a, b) != (1, 1):
+                descriptor, valid = sent(a, b)
+                pl.when(valid)(descriptor.wait_send)
+
+
+def surround(cell, number):
+    channels, width = cell.shape
+    count = width // LEAF
+    vmem = pl.BlockSpec(memory_space=pltpu.VMEM)
+    out = pl.pallas_call(
+        functools.partial(exchange, (lax.axis_size("gx"), lax.axis_size("gy"))),
+        out_shape=jax.ShapeDtypeStruct((9, channels * count, LEAF), cell.dtype),
+        in_specs=[vmem],
+        out_specs=vmem,
+        scratch_shapes=[pltpu.SemaphoreType.DMA((9,)), pltpu.SemaphoreType.DMA((9,))],
+        compiler_params=pltpu.CompilerParams(collective_id=number, has_side_effects=True),
+    )(cell.reshape(channels * count, LEAF))
+    return out.reshape(9, channels, width)
 
 
 def split3(value):
@@ -168,8 +228,8 @@
             jnp.float32(0.5),
         ]
     ).reshape(1, 3, 1)
-    own = blocks_own = base_entries // 2
-    state = surround(jnp.concatenate([position, velocity, mass], axis=2))
+    own = base_entries // 2
+    state = surround(jnp.concatenate([position, velocity, mass], axis=2)[0, 0], 0)
     pos, vel, m = state[:, 0:3], state[:, 3:6], state[:, 6:7]
     x1 = pos - centre
     x2 = (pos + 0.5 * time_step * vel) - centre
@@ -178,7 +238,7 @@
     rho1, rho2 = all_sums(tables, [x1, x2], [mass_rows, mass_rows])
     own_m = mass[0, 0]
     q_own = 1.0 / (own_m + jnp.concatenate([rho1[0:1], rho2[0:1]], axis=0))
-    q_all = surround(q_own[None, None])
+    q_all = surround(q_own, 1)
 
     def acceleration(x, v, own_v, q, own_q):
         mq = m * q
@@ -193,7 +253,7 @@
     own_v = velocity[0, 0]
     acc1 = acceleration(x1, vel, own_v, q_all[:, 0:1], q_own[0:1])
     mid_velocity = own_v + 0.5 * time_step * acc1
-    mid_all = surround(mid_velocity[None, None])
+    mid_all = surround(mid_velocity, 2)
     acc2 = acceleration(x2, mid_all, mid_velocity, q_all[:, 1:2], q_own[1:2])
     return (
         (time_step * mid_velocity)[None, None],

time: 159 us -> 136 us (0.86)
  starting transfers between devices: 37.1 us -> 0 us
  Pallas kernels: 75.3 us -> 108 us
  waiting for transfers between devices: 19.3 us -> 0 us
  local copies, waits for them, and re-layouts: 7.74 us -> 11.6 us
  other arithmetic: 15.9 us -> 13.7 us
    ppermute x12 -> x0, starting transfers between devices: 37.1 us -> none  [the longest x6 24.1 us: with_halo(): lax.ppermute(head, axis, [((i + 1) % count, i) for i in range(ends)])]
    pallas_call x0 -> x3, Pallas kernels: none -> 30.2 us  [surround(): pl.pallas_call(functools.partial(exchange, (lax.axis_size('gx'), lax.axis...]
    ppermute x12 -> x0, waiting for transfers between devices: 19.3 us -> none  [the longest x6 15.2 us: with_halo(): lax.ppermute(head, axis, [((i + 1) % count, i) for i in range(ends)])]
    reshape x0 -> x2, local copies, waits for them, and re-layouts: none -> 2.5 us  [surround(): return out.reshape(9, channels, width)]
    pallas_call x3, Pallas kernels: 75.3 us -> 77.7 us  [all_sums(): pl.pallas_call(functools.partial(pair_sums, sections, (base_items, base_e...]
    slice x0 -> x4, local copies, waits for them, and re-layouts: none -> 1.87 us  [the longest x2 1.01 us: acceleration(): s[1:4]]
    concatenate x6 -> x1, other arithmetic: 3.4 us -> 1.6 us  [local(): jnp.concatenate([position, velocity, mass], axis=2)[0, 0]]
  transfers between devices with their start and end apart: 12 -> 0, of which waited for: 8 -> 0; matrix products, arithmetic and copies ran while one was open for 4% -> 0% of each run, Pallas kernels for 0% -> 0%
where the time goes in v2:
time: 136 us; the launch traced here: 134 us
  Pallas kernels  108 us (79%)
  other arithmetic  13.7 us (10%)
  local copies, waits for them, and re-layouts  11.6 us (9%)
    pallas_call x3, Pallas kernels, all_sums(): pl.pallas_call(functools.partial(pair_sums, sections, (base_items, base_e...  77.7 us
    pallas_call x3, Pallas kernels, surround(): pl.pallas_call(functools.partial(exchange, (lax.axis_size('gx'), lax.axis...  30.2 us
    concatenate x2, other arithmetic, acceleration(): jnp.concatenate([m, m * x, mq, mq * (viscosity * v - 2.0 / kernel_scale *...  3.12 us

profile of v2, /device:TPU:28, one launch (start us, length us, event | category | flops | bytes accessed | tf_op | source)
XLA Modules:
  0.0 134.2 jit_solution(3161044642790751734)
XLA Ops:
  0.6 1.6 %pad_maximum_fusion.2 = f32[1,1,7,4096]{3,1,2,0:T(1,128)} fusion(f32[1,1,1,4096]{3,1,2,0:T(1,128)} %bitcast.142, f32[1,1,3,4096]{3,1,2,0:T(1,128)} %param.6, f32[1,1,3,4096]{3,1,2,0:T(1,128)} %param.5), kind=kLoop, calls=%fused_computation.19 | loop fusion | flops 57344 | bytes 229376 | tf_op jit(solution)/shard_map/concatenate | solution.py:232
  2.2 12.9 %shard_map.68 = f32[9,224,128]{2,1,0:T(8,128)} custom-call(f32[224,128]{1,0:T(8,128)} %bitcast.136), custom_call_target="tpu_custom_call" | custom-call | tf_op jit(solution)/shard_map/pallas_call | solution.py:90
  15.2 1.4 %reshape.360 = f32[9,7,4096]{2,1,0:T(8,128)S(1)} reshape(f32[9,224,128]{2,1,0:T(8,128)} %shard_map.68) | data formatting | bytes 2064384 | tf_op jit(solution)/shard_map/reshape | solution.py:98
  16.9 1.7 %broadcast_multiply_fusion.1 = (f32[9,3,4096]{2,1,0:T(4,128)S(1)}, f32[9,3,4096]{2,1,0:T(4,128)}, f32[9,3,4096]{2,1,0:T(4,128)S(1)}, f32[9,3,4096]{2,1,0:T(4,128)}) fusion(f32[9,4096]{1,0:T(8,128)S(1)} %bitcast.131, f32[3]{0:T(128)S(1)} %pad_maximum_fusion.4, f32[9,7,4096]{2,1,0:T(8,128)S(1)} %reshape.360), kind=kLoop, calls=%fused_computation.12 | loop fusion | flops 663552 | bytes 2801676 | tf_op jit(solution)/shard_map/mul | solution.py:245
  18.6 1.1 concatenate.26.refs_2_.refs_3_
  20.9 0.7 pad_add_fusion.src_ref
  21.5 0.7 fusion.25
  22.9 37.8 %shard_map.69 = (f32[32,8,128]{2,1,0:T(8,128)}, f32[32,8,128]{2,1,0:T(8,128)}) custom-call(s32[432]{0:T(512)} %pad_add_fusion.src_ref, s32[48]{0:T(128)} %pad_add_fusion.1.leaf_ref, s32[1]{0:T(128)} %bitcast.4.live_ref, f32[9,3,4096]{2,1,0:T(4,128)} %get-tuple-element.15.refs_0_, f32[9,3,4096]{2,1,0:T(4,128)} %get-tuple-element.19.refs_1_.refs_0_, ...), custom_call_target="tpu_custom_call" | custom-call | tf_op jit(solution)/shard_map/pallas_call | solution.py:194
  60.7 1.0 slice_bitcast_fusion.3
  63.0 8.3 %shard_map.70 = f32[9,64,128]{2,1,0:T(8,128)} custom-call(f32[64,128]{1,0:T(8,128)} %fusion.24.own_ref), custom_call_target="tpu_custom_call" | custom-call | tf_op jit(solution)/shard_map/pallas_call | solution.py:90
  71.4 1.1 reshape.361
  73.3 1.6 %fusion.1.refs_1_ = f32[9,8,4096]{2,1,0:T(8,128)} fusion(f32[9,1,4096]{2,1,0:T(1,128)S(1)} %slice.126, f32[9,3,4096]{2,1,0:T(4,128)S(1)} %subtract_multiply_fusion.1, f32[9,1,4096]{2,1,0:T(1,128)S(1)} %get-tuple-element.17, f32[9,3,4096]{2,1,0:T(4,128)S(1)} %get-tuple-element.14), kind=kLoop, calls=%fused_computation.4 | loop fusion | flops 884736 | bytes 2359296 | tf_op jit(solution)/shard_map/concatenate | solution.py:245
  74.8 20.0 %shard_map.71 = f32[32,8,128]{2,1,0:T(8,128)} custom-call(s32[432]{0:T(512)} %pad_add_fusion.src_ref, s32[48]{0:T(128)} %pad_add_fusion.1.leaf_ref, s32[1]{0:T(128)} %bitcast.4.live_ref, f32[9,3,4096]{2,1,0:T(4,128)} %get-tuple-element.15.refs_0_, f32[9,8,4096]{2,1,0:T(8,128)} %fusion.1.refs_1_), custom_call_target="tpu_custom_call" | custom-call | tf_op jit(solution)/shard_map/pallas_call | solution.py:194
  94.8 1.0 fusion.29
  95.8 1.0 fusion.28
  96.9 0.9 slice.130
  98.5 8.9 %shard_map.72 = f32[9,96,128]{2,1,0:T(8,128)} custom-call(f32[96,128]{1,0:T(8,128)} %fusion.19.own_ref), custom_call_target="tpu_custom_call" | custom-call | tf_op jit(solution)/shard_map/pallas_call | solution.py:90
  107.4 1.1 broadcast_multiply_fusion.2
  109.1 1.6 %fusion.3.refs_1_ = f32[9,8,4096]{2,1,0:T(8,128)} fusion(f32[9,1,4096]{2,1,0:T(1,128)S(1)} %slice.126, f32[9,3,4096]{2,1,0:T(4,128)S(1)} %subtract_multiply_fusion, f32[9,1,4096]{2,1,0:T(1,128)S(1)} %get-tuple-element.16, f32[9,3,4096]{2,1,0:T(4,128)S(1)} %get-tuple-element.18), kind=kLoop, calls=%fused_computation.6 | loop fusion | flops 884736 | bytes 2359296 | tf_op jit(solution)/shard_map/concatenate | solution.py:245
  110.6 20.0 %shard_map.73 = f32[32,8,128]{2,1,0:T(8,128)} custom-call(s32[432]{0:T(512)} %pad_add_fusion.src_ref, s32[48]{0:T(128)} %pad_add_fusion.1.leaf_ref, s32[1]{0:T(128)} %bitcast.4.live_ref, f32[9,3,4096]{2,1,0:T(4,128)} %get-tuple-element.19.refs_1_.refs_0_, f32[9,8,4096]{2,1,0:T(8,128)} %fusion.3.refs_1_), custom_call_target="tpu_custom_call" | custom-call | tf_op jit(solution)/shard_map/pallas_call | solution.py:194
  130.6 1.0 fusion.27
  131.7 1.2 copy_add_fusion
  132.8 0.7 copy.24
  133.5 0.7 copy.25
  (53 shorter events, 5.5 us)
Async XLA Ops:
  18.6 1.1 copy-start.6
  18.6 1.3 %copy-start.7 = (s32[1,1,8]{2,1,0:T(1,128)S(1)}, s32[1,1,8]{2,1,0:T(1,128)}, u32[]{:S(2)}) copy-start(s32[1,1,8]{2,1,0:T(1,128)} %param.9) | copy-start | bytes 100
  22.9 38.8 %copy-start.4 = (f32[1,1,1,4096]{3,2,1,0:T(1,128)S(1)}, f32[1,1,1,4096]{3,2,1,0:T(1,128)}, u32[]{:S(2)}) copy-start(f32[1,1,1,4096]{3,2,1,0:T(1,128)} %param.7) | copy-start | bytes 49156
  61.7 11.2 %copy-start = (f32[9,3,4096]{2,1,0:T(4,128)S(1)}, f32[9,3,4096]{2,1,0:T(4,128)}, u32[]{:S(2)}) copy-start(f32[9,3,4096]{2,1,0:T(4,128)} %get-tuple-element.15.refs_0_) | copy-start | bytes 1327108
  74.8 22.0 %copy-start.5 = (f32[2,4096]{1,0:T(2,128)S(1)}, f32[2,4096]{1,0:T(2,128)}, u32[]{:S(2)}) copy-start(f32[2,4096]{1,0:T(2,128)} %get-tuple-element.28) | copy-start | bytes 98308
  74.8 23.0 %copy-start.3 = (f32[1,1,3,4096]{3,1,2,0:T(1,128)S(1)}, f32[1,1,3,4096]{3,1,2,0:T(1,128)}, u32[]{:S(2)}) copy-start(f32[1,1,3,4096]{3,1,2,0:T(1,128)} %param.6) | copy-start | bytes 147460
  107.4 1.4 %copy-start.1 = (f32[9,3,4096]{2,1,0:T(4,128)S(1)}, f32[9,3,4096]{2,1,0:T(4,128)}, u32[]{:S(2)}) copy-start(f32[9,3,4096]{2,1,0:T(4,128)} %get-tuple-element.19.refs_1_.refs_0_) | copy-start | bytes 1327108
  110.6 21.0 %copy-start.2 = (f32[32,8,128]{2,1,0:T(8,128)S(1)}, f32[32,8,128]{2,1,0:T(8,128)}, u32[]{:S(2)}) copy-start(f32[32,8,128]{2,1,0:T(8,128)} %shard_map.71) | copy-start | bytes 393220
